TPU v7x, 32 devices: a whole 2x2x4 slice. The times are simulated.
32 devices in a mesh: gx: 4 (over y, x), gy: 2 (over core), gz: 4 (over z).
Axes of the slice: x: 2, y: 2, z: 4, core: 2. Of those that a mesh axis runs over, the one named last changes fastest.
Arguments:
- start_block: float32 [64, 3, 8, 16, 512], P(None, None, 'gx', 'gy', 'gz'), may hold values from -6 to 6
- stiff_field: float32 [8, 16, 512], P('gx', 'gy', 'gz'), may hold values from 0.5 to 2
- shift_field: float32 [8, 16, 512], P('gx', 'gy', 'gz'), may hold values from 0.25 to 2
- mass_field: float32 [8, 16, 512], P('gx', 'gy', 'gz'), may hold values from 0.5 to 2
Outputs:
- modes: float32 [64, 3, 8, 16, 512], P(None, None, 'gx', 'gy', 'gz')
- ritz: float32 [64, 64], replicated
All inputs are finite; a program needn't handle non-finite values. Where the computation divides by a largest or mean magnitude, that divisor is 1e-20 or more.
Results may differ from a plain program's by a relative error of at most 0.0003.
Values sent between devices are 32-bit elements; how exact they have to be, the bound alone decides.
A program may use at most 128 MiB of HBM per device.

v0:
```python
import jax
import jax.numpy as jnp
from jax import lax
from jax.sharding import PartitionSpec as P

ITERS = 2
FILTER = 4


def with_halo(x, sides, width):
    for axis, dim in sides:
        devices, length = (lax.axis_size(axis), x.shape[dim])
        up = [(i, (i + 1) % devices) for i in range(devices - 1)]
        down = [(j, i) for i, j in up]
        last = lax.slice_in_dim(x, length - width, length, axis=dim)
        initial = lax.slice_in_dim(x, 0, width, axis=dim)
        before = lax.ppermute(last, axis, up)
        after = lax.ppermute(initial, axis, down)
        x = jnp.concatenate([before, x, after], axis=dim)
    return x


def lower_solve(lower_mat, rhs):
    return lax.linalg.triangular_solve(lower_mat, rhs, left_side=True, lower=True)


def lower_trans_solve(lower_mat, rhs):
    return lax.linalg.triangular_solve(lower_mat, rhs, left_side=True, lower=True, transpose_a=True)


def hidot(left, right):
    return jnp.dot(left, right, precision=lax.Precision.HIGHEST, preferred_element_type=jnp.float32)


def gram_of(left, right):
    return hidot(left.reshape(left.shape[0], -1), right.reshape(right.shape[0], -1).T)


def combine(coeffs, vectors):
    flat = hidot(coeffs.T, vectors.reshape(vectors.shape[0], -1))
    return flat.reshape((coeffs.shape[1],) + vectors.shape[1:])


def crop_one(field):
    return field[..., 1:-1, 1:-1, 1:-1]


def offset_view(field, step_x, step_y, step_z):
    size_x, size_y, size_z = (field.shape[-3], field.shape[-2], field.shape[-1])
    return field[
        ...,
        1 + step_x : size_x - 1 + step_x,
        1 + step_y : size_y - 1 + step_y,
        1 + step_z : size_z - 1 + step_z,
    ]


def stiffness_local(padded_field, padded_stiff, center_stiff, center_shift):
    interior = crop_one(padded_field)
    offsets = ((1, 0, 0), (-1, 0, 0), (0, 1, 0), (0, -1, 0), (0, 0, 1), (0, 0, -1))
    beside_all = None
    for step_x, step_y, step_z in offsets:
        term = offset_view(padded_stiff, step_x, step_y, step_z) * offset_view(
            padded_field, step_x, step_y, step_z
        )
        beside_all = term if beside_all is None else beside_all + term
    laplace = 6.0 * (crop_one(padded_stiff) * interior) - beside_all
    summed = jnp.sum(interior, axis=1, keepdims=True)
    return center_stiff * laplace + center_shift * (interior + 0.5 * summed)


def ritz_filter(pencil_k, pencil_m, mode_count):
    factor = jnp.linalg.cholesky(pencil_m)
    partial_value = lower_solve(factor, pencil_k)
    reduced = lower_solve(factor, partial_value.T).T
    gershgorin = jnp.max(jnp.sum(jnp.abs(reduced), axis=1))
    search = factor.T[:, :mode_count]
    for sweep_index in range(FILTER):
        search = search - hidot(reduced, search) / gershgorin
    correlation = hidot(search.T, search)
    small_factor = jnp.linalg.cholesky(correlation)
    orthonormal = lower_solve(small_factor, search.T).T
    coeffs = lower_trans_solve(factor, orthonormal)
    ritz_matrix = hidot(orthonormal.T, hidot(reduced, orthonormal))
    return (coeffs, ritz_matrix)


def start_sums(start_block, mass_field, start_image, dof_count):
    mass_gram, stiff_gram = lax.psum(
        (gram_of(start_block, mass_field * start_block), gram_of(start_block, start_image)),
        ("gx", "gy", "gz"),
    )
    return (mass_gram / dof_count, stiff_gram / dof_count)


def normalize(factor, field):
    return lower_solve(factor, field.reshape(field.shape[0], -1)).reshape(field.shape)


def local(start_block, stiff_field, shift_field, mass_field):
    count = start_block.shape[0]
    dof_count = (
        3.0 * stiff_field.size * lax.axis_size("gx") * lax.axis_size("gy") * lax.axis_size("gz")
    )
    joined = jnp.stack([stiff_field, shift_field, mass_field])
    padded_coef = with_halo(joined, (("gx", 1), ("gy", 2), ("gz", 3)), 2)
    wide_coef = crop_one(padded_coef)
    diagonal = 6.0 * stiff_field * stiff_field + 1.5 * shift_field

    def apply_stiff(field):
        padded = with_halo(field, (("gx", 2), ("gy", 3), ("gz", 4)), 1)
        return stiffness_local(padded, wide_coef[0], stiff_field, shift_field)

    start_image = apply_stiff(start_block)
    mass_gram, stiff_gram = start_sums(start_block, mass_field, start_image, dof_count)
    factor = jnp.linalg.cholesky(mass_gram)
    current = normalize(factor, start_block)
    stiff_image = normalize(factor, start_image)
    ritz_matrix = lower_solve(factor, lower_solve(factor, stiff_gram).T).T
    residual = (stiff_image - mass_field * combine(ritz_matrix, current)) / diagonal
    stiff_resid = apply_stiff(residual)
    previous = None
    for iteration in range(ITERS):
        if iteration > 0:
            residual = (stiff_image - mass_field * combine(ritz_matrix, current)) / diagonal
            stiff_resid = apply_stiff(residual)
            search_set = jnp.concatenate([current, residual, previous[0]], axis=0)
            image_set = jnp.concatenate([stiff_image, stiff_resid, previous[1]], axis=0)
        else:
            search_set = jnp.concatenate([current, residual], axis=0)
            image_set = jnp.concatenate([stiff_image, stiff_resid], axis=0)
        pencil_k, pencil_m = lax.psum(
            (gram_of(search_set, image_set), gram_of(search_set, mass_field * search_set)),
            ("gx", "gy", "gz"),
        )
        coeffs, ritz_matrix = ritz_filter(pencil_k / dof_count, pencil_m / dof_count, count)
        current = combine(coeffs, search_set)
        stiff_image = combine(coeffs, image_set)
        previous = (
            combine(coeffs[count:], search_set[count:]),
            combine(coeffs[count:], image_set[count:]),
        )
    return (current, ritz_matrix)


def solution(mesh):
    in_specs = (
        P(None, None, "gx", "gy", "gz"),
        P("gx", "gy", "gz"),
        P("gx", "gy", "gz"),
        P("gx", "gy", "gz"),
    )
    out_specs = (P(None, None, "gx", "gy", "gz"), P())
    return jax.shard_map(local, mesh=mesh, in_specs=in_specs, out_specs=out_specs, check_vma=False)
```

profile of v0, /device:TPU:0, one launch (start us, length us, event | category | flops | bytes accessed | tf_op | source)
XLA Modules:
  0.0 744.3 jit_solution(5422652426399144735)
XLA Ops:
  7.9 4.9 collective-permute-start
  17.3 5.4 collective-permute-start.7
  26.3 2.3 fusion.96
  33.1 5.3 collective-permute-done.7
  40.1 18.0 %collective-permute-done.6 = f32[64,3,1,8,128]{4,0,3,2,1:T(8,128)} collective-permute-done((f32[64,3,1,8,128]{4,0,3,2,1:T(8,128)}, f32[64,3,1,8,128]{4,0,3,2,1:T(8,128)}, u32[]{:S(2)}, u32[]{:S(2)}) %collective-permute-start.6) | collective-permute-done | bytes 786464 | tf_op jit(solution)/shard_map/ppermute | solution.py:18
  60.8 3.1 collective-permute-start.9
  64.0 3.5 collective-permute-start.4
  70.1 4.4 collective-permute-done.5
  76.6 4.4 fusion.183
  81.1 3.4 copy.129
  85.8 3.4 copy.131
  89.2 5.4 collective-permute-start.11
  96.4 3.4 copy.130
  99.8 3.4 copy.132
  103.1 5.7 fusion.61
  112.7 40.4 %all-reduce.5 = (f32[64,64]{0,1:T(8,128)S(1)}, f32[64,64]{0,1:T(8,128)S(1)}) all-reduce(f32[64,64]{0,1:T(8,128)S(1)} %copy-done.35, f32[64,64]{0,1:T(8,128)S(1)} %convolution_bitcast_fusion.3), channel_id=1, replica_groups=mesh['gx'=4,'gy'=2,'gz'=4] {'gx','gy','gz'}, use_global_device_ids=true, to_apply=%region_0.0 | all-reduce | flops 8192 | bytes 65536 | tf_op jit(solution)/shard_map/psum | solution.py:89
  153.2 5.8 cholesky.214
  160.4 4.9 custom-call.49
  169.3 3.2 subtract_divide_fusion
  174.0 3.3 fusion.179
  178.8 4.8 collective-permute-start.13
  183.7 16.4 %collective-permute-done.12 = f32[64,3,1,8,128]{4,0,3,2,1:T(8,128)S(1)} collective-permute-done((f32[64,3,1,8,128]{4,0,3,2,1:T(8,128)S(1)}, f32[64,3,1,8,128]{4,0,3,2,1:T(8,128)S(1)}, u32[]{:S(2)}, u32[]{:S(2)}) %collective-permute-start.12) | collective-permute-done | bytes 786464 | tf_op jit(solution)/shard_map/ppermute | solution.py:18
  201.5 3.3 collective-permute-start.15
  206.2 3.4 fusion.89
  210.8 4.4 fusion.182
  215.2 3.4 copy.142
  219.9 3.4 copy.144
  223.3 5.3 collective-permute-start.17
  232.4 3.4 copy.143
  235.8 3.4 copy.145
  239.2 4.3 fusion.47
  246.9 3.3 fusion.86
  250.3 3.9 maximum_bitcast_fusion.1
  254.1 4.0 copy.188
  259.6 128.5 %all-reduce.13.cloned.1.call-done = (f32[128,128]{0,1:T(8,128)}, f32[128,128]{0,1:T(8,128)}) async-done(((f32[128,128]{0,1:T(8,128)}, f32[128,128]{0,1:T(8,128)}), (f32[128,128]{0,1:T(8,128)}, f32[128,128]{0,1:T(8,128)})) %all-reduce.13.cloned.1.call-update) | async-done | bytes 131088 | tf_op jit(solution)/shard_map/psum | solution.py:132
  389.9 11.7 %cholesky.95 = f32[128,128]{1,0:T(8,128)S(1)} custom-call(f32[128,128]{1,0:T(8,128)S(1)} %fusion.124), custom_call_target="Cholesky" | custom-call | tf_op jit(solution)/shard_map/jit(cholesky)/cholesky | solution.py:73
  403.0 9.8 %custom-call.40 = f32[1,128,128]{1,2,0:T(8,128)S(1)} custom-call(f32[1,128,128]{2,1,0:T(8,128)S(1)} %get-tuple-element.101), custom_call_target="InvertDiagBlocksLowerTriangular" | custom-call | tf_op jit(solution)/shard_map/triangular_solve | solution.py:28
  418.5 5.8 cholesky.225
  425.7 4.9 custom-call.41
  436.8 5.9 fusion.177
  445.0 4.6 collective-permute-start.19
  452.4 2.7 copy_bitcast_fusion
  456.8 3.0 fusion.71
  459.9 6.2 collective-permute-done.18
  467.4 3.3 collective-permute-start.21
  470.7 4.8 fusion.83
  476.4 4.4 fusion.181
  480.8 3.4 copy.158
  485.5 3.4 copy.160
  489.0 5.2 collective-permute-start.23
  496.5 3.4 copy.159
  499.9 3.4 copy.161
  503.3 4.6 fusion.33
  507.9 4.6 fusion.80
  512.6 2.2 maximum_bitcast_fusion
  514.8 3.0 copy.203
  517.8 137.8 %all-reduce.11.cloned.1.call-done = (f32[192,192]{0,1:T(8,128)}, f32[192,192]{0,1:T(8,128)}) async-done(((f32[192,192]{0,1:T(8,128)}, f32[192,192]{0,1:T(8,128)}), (f32[192,192]{0,1:T(8,128)}, f32[192,192]{0,1:T(8,128)})) %all-reduce.11.cloned.1.call-update) | async-done | bytes 294928 | tf_op jit(solution)/shard_map/psum | solution.py:132
  657.7 11.7 %cholesky.155 = f32[128,128]{1,0:T(8,128)S(1)} custom-call(f32[128,128]{1,0:T(8,128)S(1)} %cholesky.245), custom_call_target="Cholesky" | custom-call | tf_op jit(solution)/shard_map/jit(cholesky)/cholesky | solution.py:73
  669.5 9.8 %custom-call.42 = f32[1,128,128]{1,2,0:T(8,128)S(1)} custom-call(f32[1,128,128]{2,1,0:T(8,128)S(1)} %get-tuple-element.99), custom_call_target="InvertDiagBlocksLowerTriangular" | custom-call | tf_op jit(solution)/shard_map/jit(cholesky)/cholesky | solution.py:73
  679.7 6.0 cholesky.169
  688.5 19.7 %custom-call.43 = f32[2,128,128]{1,2,0:T(8,128)S(1)} custom-call(f32[2,128,128]{2,1,0:T(8,128)S(1)} %pad_maximum_fusion.72), custom_call_target="InvertDiagBlocksLowerTriangular" | custom-call | tf_op jit(solution)/shard_map/triangular_solve | solution.py:28
  714.9 5.8 cholesky.236
  722.1 4.9 custom-call.44
  729.0 6.2 fusion.10
  (237 shorter events, 96.3 us)
Async XLA Ops:
  7.2 381.0 %all-reduce.13.cloned.1.call-start = ((), (), s32[]{:S(2)}) async-start(), calls=%async_computation.1 | async-start | bytes 262144 | tf_op jit(solution)/shard_map/psum | solution.py:132
  7.9 20.6 %collective-permute-start = (f32[3,2,8,128]{3,2,1,0:T(8,128)S(1)}, f32[3,2,8,128]{3,2,1,0:T(8,128)S(1)}, u32[]{:S(2)}, u32[]{:S(2)}) collective-permute-start(f32[3,2,8,128]{3,2,1,0:T(8,128)S(1)} %pad_maximum_fusion.78), channel_id=1, source_target_pairs={{0,8},{8,16},{16,24},{1,9},{9,17},{17,25},{2,10},{10,18},{18,26},{... | collective-permute-start | bytes 73736 | tf_op jit(solution)/shard_map/ppermute | solution.py:17
  12.8 15.8 %collective-permute-start.1 = (f32[3,2,8,128]{3,2,1,0:T(8,128)S(1)}, f32[3,2,8,128]{3,2,1,0:T(8,128)S(1)}, u32[]{:S(2)}, u32[]{:S(2)}) collective-permute-start(f32[3,2,8,128]{3,2,1,0:T(8,128)S(1)} %pad_maximum_fusion.78), channel_id=1, source_target_pairs={{8,0},{16,8},{24,16},{9,1},{17,9},{25,17},{10,2},{18,10},{26,18},{... | collective-permute-start | bytes 73736 | tf_op jit(solution)/shard_map/ppermute | solution.py:18
  16.0 8.1 %copy-start = (f32[64,3,2,8,128]{4,3,2,1,0:T(8,128)S(1)}, f32[64,3,2,8,128]{4,3,2,1,0:T(8,128)}, u32[]{:S(2)}) copy-start(f32[64,3,2,8,128]{4,3,2,1,0:T(8,128)} %param.13) | copy-start | bytes 4718596
  17.3 21.1 %collective-permute-start.7 = (f32[64,3,1,8,128]{4,0,3,2,1:T(8,128)}, f32[64,3,1,8,128]{4,0,3,2,1:T(8,128)}, u32[]{:S(2)}, u32[]{:S(2)}) collective-permute-start(f32[64,3,1,8,128]{4,0,3,2,1:T(8,128)} %get-tuple-element.91), channel_id=1, source_target_pairs={{0,8},{8,16},{16,24},{1,9},{9,17},{17,25},{2,10},{10,18},{18,26},{... | collective-permute-start | bytes 2359304 | tf_op jit(solution)/shard_map/ppermute | solution.py:17
  22.7 3.5 copy-start.26
  22.7 35.4 %collective-permute-start.6 = (f32[64,3,1,8,128]{4,0,3,2,1:T(8,128)}, f32[64,3,1,8,128]{4,0,3,2,1:T(8,128)}, u32[]{:S(2)}, u32[]{:S(2)}) collective-permute-start(f32[64,3,1,8,128]{4,0,3,2,1:T(8,128)} %get-tuple-element.90), channel_id=1, source_target_pairs={{8,0},{16,8},{24,16},{9,1},{17,9},{25,17},{10,2},{18,10},{26,18},{... | collective-permute-start | bytes 2359304 | tf_op jit(solution)/shard_map/ppermute | solution.py:18
  26.2 2.4 copy-start.27
  26.3 2.3 copy-start.28
  28.6 11.5 %copy-start.31 = (f32[3,2,8,128]{3,2,1,0:T(8,128)}, f32[3,2,8,128]{3,2,1,0:T(8,128)S(1)}, u32[]{:S(2)}) copy-start(f32[3,2,8,128]{3,2,1,0:T(8,128)S(1)} %collective-permute-done) | copy-start | bytes 73732
  28.6 11.5 %copy-start.33 = (f32[3,2,8,128]{3,2,1,0:T(8,128)}, f32[3,2,8,128]{3,2,1,0:T(8,128)S(1)}, u32[]{:S(2)}) copy-start(f32[3,2,8,128]{3,2,1,0:T(8,128)S(1)} %collective-permute-done.1) | copy-start | bytes 73732
  28.6 3.2 collective-permute-start.2
  29.9 3.1 collective-permute-start.3
  59.3 16.0 %copy-start.5 = (f32[64,3,4,8,128]{4,0,3,2,1:T(8,128)}, f32[64,3,4,8,128]{4,0,3,2,1:T(8,128)S(1)}, u32[]{:S(2)}) copy-start(f32[64,3,4,8,128]{4,0,3,2,1:T(8,128)S(1)} %constant_dynamic-update-slice_fusion) | copy-start | bytes 9437188
  59.3 15.2 %copy-start.32 = (f32[3,2,8,128]{3,2,1,0:T(8,128)S(1)}, f32[3,2,8,128]{3,2,1,0:T(8,128)}, u32[]{:S(2)}) copy-start(f32[3,2,8,128]{3,2,1,0:T(8,128)} %copy-done.31) | copy-start | bytes 73732
  59.3 15.2 %copy-start.34 = (f32[3,2,8,128]{3,2,1,0:T(8,128)S(1)}, f32[3,2,8,128]{3,2,1,0:T(8,128)}, u32[]{:S(2)}) copy-start(f32[3,2,8,128]{3,2,1,0:T(8,128)} %copy-done.33) | copy-start | bytes 73732
  59.4 15.9 %collective-permute-start.8 = (f32[64,3,4,1,128]{4,0,3,2,1:T(8,128)S(1)}, f32[64,3,4,1,128]{4,0,3,2,1:T(8,128)S(1)}, u32[]{:S(2)}, u32[]{:S(2)}) collective-permute-start(f32[64,3,4,1,128]{4,0,3,2,1:T(8,128)S(1)} %get-tuple-element.82), channel_id=1, source_target_pairs={{4,0},{5,1},{6,2},{7,3},{12,8},{13,9},{14,10},{15,11},{20,16},{21,... | collective-permute-start | bytes 1179656 | tf_op jit(solution)/shard_map/ppermute | solution.py:18
  60.8 14.5 %collective-permute-start.9 = (f32[64,3,4,1,128]{4,0,3,2,1:T(8,128)S(1)}, f32[64,3,4,1,128]{4,0,3,2,1:T(8,128)S(1)}, u32[]{:S(2)}, u32[]{:S(2)}) collective-permute-start(f32[64,3,4,1,128]{4,0,3,2,1:T(8,128)S(1)} %get-tuple-element.81), channel_id=1, source_target_pairs={{0,4},{1,5},{2,6},{3,7},{8,12},{9,13},{10,14},{11,15},{16,20},{17,... | collective-permute-start | bytes 1179656 | tf_op jit(solution)/shard_map/ppermute | solution.py:17
  64.0 6.1 collective-permute-start.4
  67.5 7.0 collective-permute-start.5
  75.3 0.8 copy-start.25
  84.5 11.9 %collective-permute-start.10 = (f32[64,3,4,10,1]{0,2,4,3,1:T(4,128)}, f32[64,3,4,10,1]{0,2,4,3,1:T(4,128)}, u32[]{:S(2)}, u32[]{:S(2)}) collective-permute-start(f32[64,3,4,10,1]{0,2,4,3,1:T(4,128)} %copy.129), channel_id=1, source_target_pairs={{1,0},{2,1},{3,2},{5,4},{6,5},{7,6},{9,8},{10,9},{11,10},{13,12},{... | collective-permute-start | bytes 92168 | tf_op jit(solution)/shard_map/ppermute | solution.py:18
  89.2 10.5 %collective-permute-start.11 = (f32[64,3,4,10,1]{0,2,4,3,1:T(4,128)}, f32[64,3,4,10,1]{0,2,4,3,1:T(4,128)}, u32[]{:S(2)}, u32[]{:S(2)}) collective-permute-start(f32[64,3,4,10,1]{0,2,4,3,1:T(4,128)} %copy.131), channel_id=1, source_target_pairs={{0,1},{1,2},{2,3},{4,5},{5,6},{6,7},{8,9},{9,10},{10,11},{12,13},{... | collective-permute-start | bytes 92168 | tf_op jit(solution)/shard_map/ppermute | solution.py:17
  110.6 2.1 copy-start.35
  167.7 1.5 copy-start.36
  167.7 1.6 copy-start.17
  172.5 1.2 copy-start.9
  177.5 22.6 %collective-permute-start.12 = (f32[64,3,1,8,128]{4,0,3,2,1:T(8,128)S(1)}, f32[64,3,1,8,128]{4,0,3,2,1:T(8,128)S(1)}, u32[]{:S(2)}, u32[]{:S(2)}) collective-permute-start(f32[64,3,1,8,128]{4,0,3,2,1:T(8,128)S(1)} %get-tuple-element.89), channel_id=1, source_target_pairs={{8,0},{16,8},{24,16},{9,1},{17,9},{25,17},{10,2},{18,10},{26,18},{... | collective-permute-start | bytes 2359304 | tf_op jit(solution)/shard_map/ppermute | solution.py:18
  178.8 21.3 %collective-permute-start.13 = (f32[64,3,1,8,128]{4,0,3,2,1:T(8,128)S(1)}, f32[64,3,1,8,128]{4,0,3,2,1:T(8,128)S(1)}, u32[]{:S(2)}, u32[]{:S(2)}) collective-permute-start(f32[64,3,1,8,128]{4,0,3,2,1:T(8,128)S(1)} %get-tuple-element.88), channel_id=1, source_target_pairs={{0,8},{8,16},{16,24},{1,9},{9,17},{17,25},{2,10},{10,18},{18,26},{... | collective-permute-start | bytes 2359304 | tf_op jit(solution)/shard_map/ppermute | solution.py:17
  200.1 9.5 %copy-start.11 = (f32[64,3,1,8,128]{4,0,3,2,1:T(8,128)}, f32[64,3,1,8,128]{4,0,3,2,1:T(8,128)S(1)}, u32[]{:S(2)}) copy-start(f32[64,3,1,8,128]{4,0,3,2,1:T(8,128)S(1)} %collective-permute-done.12) | copy-start | bytes 2359300
  200.1 9.5 %copy-start.12 = (f32[64,3,1,8,128]{4,0,3,2,1:T(8,128)}, f32[64,3,1,8,128]{4,0,3,2,1:T(8,128)S(1)}, u32[]{:S(2)}) copy-start(f32[64,3,1,8,128]{4,0,3,2,1:T(8,128)S(1)} %collective-permute-done.13) | copy-start | bytes 2359300
  200.2 9.4 %collective-permute-start.14 = (f32[64,3,4,1,128]{4,0,3,2,1:T(8,128)S(1)}, f32[64,3,4,1,128]{4,0,3,2,1:T(8,128)S(1)}, u32[]{:S(2)}, u32[]{:S(2)}) collective-permute-start(f32[64,3,4,1,128]{4,0,3,2,1:T(8,128)S(1)} %get-tuple-element.80), channel_id=1, source_target_pairs={{4,0},{5,1},{6,2},{7,3},{12,8},{13,9},{14,10},{15,11},{20,16},{21,... | collective-permute-start | bytes 1179656 | tf_op jit(solution)/shard_map/ppermute | solution.py:18
  201.5 8.1 %collective-permute-start.15 = (f32[64,3,4,1,128]{4,0,3,2,1:T(8,128)S(1)}, f32[64,3,4,1,128]{4,0,3,2,1:T(8,128)S(1)}, u32[]{:S(2)}, u32[]{:S(2)}) collective-permute-start(f32[64,3,4,1,128]{4,0,3,2,1:T(8,128)S(1)} %get-tuple-element.79), channel_id=1, source_target_pairs={{0,4},{1,5},{2,6},{3,7},{8,12},{9,13},{10,14},{11,15},{16,20},{17,... | collective-permute-start | bytes 1179656 | tf_op jit(solution)/shard_map/ppermute | solution.py:17
  206.2 3.4 copy-start.3
  209.6 0.7 copy-start.20
  218.6 13.8 %collective-permute-start.16 = (f32[64,3,4,10,1]{0,2,4,3,1:T(4,128)}, f32[64,3,4,10,1]{0,2,4,3,1:T(4,128)}, u32[]{:S(2)}, u32[]{:S(2)}) collective-permute-start(f32[64,3,4,10,1]{0,2,4,3,1:T(4,128)} %copy.142), channel_id=1, source_target_pairs={{1,0},{2,1},{3,2},{5,4},{6,5},{7,6},{9,8},{10,9},{11,10},{13,12},{... | collective-permute-start | bytes 92168 | tf_op jit(solution)/shard_map/ppermute | solution.py:18
  223.3 7.7 %copy-start.7 = (f32[64,6144]{1,0:T(8,128)S(1)}, f32[64,6144]{1,0:T(8,128)}, u32[]{:S(2)}) copy-start(f32[64,6144]{1,0:T(8,128)} %get-tuple-element.111) | copy-start | bytes 4718596
  223.3 12.5 %collective-permute-start.17 = (f32[64,3,4,10,1]{0,2,4,3,1:T(4,128)}, f32[64,3,4,10,1]{0,2,4,3,1:T(4,128)}, u32[]{:S(2)}, u32[]{:S(2)}) collective-permute-start(f32[64,3,4,10,1]{0,2,4,3,1:T(4,128)} %copy.144), channel_id=1, source_target_pairs={{0,1},{1,2},{2,3},{4,5},{5,6},{6,7},{8,9},{9,10},{10,11},{12,13},{... | collective-permute-start | bytes 92168 | tf_op jit(solution)/shard_map/ppermute | solution.py:17
  244.5 1.6 copy-start.4
  244.5 2.4 copy-start.18
  250.2 405.3 %all-reduce.11.cloned.1.call-start = ((), (), s32[]{:S(2)}) async-start(), calls=%async_computation | async-start | bytes 786432 | tf_op jit(solution)/shard_map/psum | solution.py:132
  254.1 4.0 copy-start.6
  259.6 171.6 %copy-start.8 = (f32[64,6144]{1,0:T(8,128)S(1)}, f32[64,6144]{1,0:T(8,128)}, u32[]{:S(2)}) copy-start(f32[64,6144]{1,0:T(8,128)} %get-tuple-element.111) | copy-start | bytes 4718596
  433.1 22.1 %copy-start.1 = (f32[64,6144]{1,0:T(8,128)}, f32[64,6144]{1,0:T(8,128)S(1)}, u32[]{:S(2)}) copy-start(f32[64,6144]{1,0:T(8,128)S(1)} %fusion.16) | copy-start | bytes 4718596
  433.3 2.0 copy-start.37
  434.9 1.9 copy-start.10
  442.8 6.8 copy-start.13
  443.7 22.3 %collective-permute-start.18 = (f32[64,3,1,8,128]{4,0,3,2,1:T(8,128)S(1)}, f32[64,3,1,8,128]{4,0,3,2,1:T(8,128)S(1)}, u32[]{:S(2)}, u32[]{:S(2)}) collective-permute-start(f32[64,3,1,8,128]{4,0,3,2,1:T(8,128)S(1)} %get-tuple-element.84), channel_id=1, source_target_pairs={{8,0},{16,8},{24,16},{9,1},{17,9},{25,17},{10,2},{18,10},{26,18},{... | collective-permute-start | bytes 2359304 | tf_op jit(solution)/shard_map/ppermute | solution.py:18
  445.0 21.0 %collective-permute-start.19 = (f32[64,3,1,8,128]{4,0,3,2,1:T(8,128)S(1)}, f32[64,3,1,8,128]{4,0,3,2,1:T(8,128)S(1)}, u32[]{:S(2)}, u32[]{:S(2)}) collective-permute-start(f32[64,3,1,8,128]{4,0,3,2,1:T(8,128)S(1)} %get-tuple-element.83), channel_id=1, source_target_pairs={{0,8},{8,16},{16,24},{1,9},{9,17},{17,25},{2,10},{10,18},{18,26},{... | collective-permute-start | bytes 2359304 | tf_op jit(solution)/shard_map/ppermute | solution.py:17
  451.5 19.2 %copy-start.15 = (f32[64,3,2,8,128]{4,0,3,2,1:T(8,128)}, f32[64,3,2,8,128]{4,0,3,2,1:T(8,128)S(1)}, u32[]{:S(2)}) copy-start(f32[64,3,2,8,128]{4,0,3,2,1:T(8,128)S(1)} %fusion.73) | copy-start | bytes 4718596
  455.4 1.4 copy-start.14
  455.9 14.8 %copy-start.22 = (f32[64,3,2,8,128]{4,0,3,2,1:T(8,128)}, f32[64,3,2,8,128]{4,0,3,2,1:T(8,128)S(1)}, u32[]{:S(2)}) copy-start(f32[64,3,2,8,128]{4,0,3,2,1:T(8,128)S(1)} %copy.155) | copy-start | bytes 4718596
  466.1 9.4 %collective-permute-start.20 = (f32[64,3,4,1,128]{4,0,3,2,1:T(8,128)S(1)}, f32[64,3,4,1,128]{4,0,3,2,1:T(8,128)S(1)}, u32[]{:S(2)}, u32[]{:S(2)}) collective-permute-start(f32[64,3,4,1,128]{4,0,3,2,1:T(8,128)S(1)} %get-tuple-element.78), channel_id=1, source_target_pairs={{4,0},{5,1},{6,2},{7,3},{12,8},{13,9},{14,10},{15,11},{20,16},{21,... | collective-permute-start | bytes 1179656 | tf_op jit(solution)/shard_map/ppermute | solution.py:18
  467.4 8.1 %collective-permute-start.21 = (f32[64,3,4,1,128]{4,0,3,2,1:T(8,128)S(1)}, f32[64,3,4,1,128]{4,0,3,2,1:T(8,128)S(1)}, u32[]{:S(2)}, u32[]{:S(2)}) collective-permute-start(f32[64,3,4,1,128]{4,0,3,2,1:T(8,128)S(1)} %get-tuple-element.77), channel_id=1, source_target_pairs={{0,4},{1,5},{2,6},{3,7},{8,12},{9,13},{10,14},{11,15},{16,20},{17,... | collective-permute-start | bytes 1179656 | tf_op jit(solution)/shard_map/ppermute | solution.py:17
  475.5 0.9 copy-start.21
  484.2 12.2 %collective-permute-start.22 = (f32[64,3,4,10,1]{0,2,4,3,1:T(4,128)}, f32[64,3,4,10,1]{0,2,4,3,1:T(4,128)}, u32[]{:S(2)}, u32[]{:S(2)}) collective-permute-start(f32[64,3,4,10,1]{0,2,4,3,1:T(4,128)} %copy.158), channel_id=1, source_target_pairs={{1,0},{2,1},{3,2},{5,4},{6,5},{7,6},{9,8},{10,9},{11,10},{13,12},{... | collective-permute-start | bytes 92168 | tf_op jit(solution)/shard_map/ppermute | solution.py:18
  489.0 10.9 %collective-permute-start.23 = (f32[64,3,4,10,1]{0,2,4,3,1:T(4,128)}, f32[64,3,4,10,1]{0,2,4,3,1:T(4,128)}, u32[]{:S(2)}, u32[]{:S(2)}) collective-permute-start(f32[64,3,4,10,1]{0,2,4,3,1:T(4,128)} %copy.160), channel_id=1, source_target_pairs={{0,1},{1,2},{2,3},{4,5},{5,6},{6,7},{8,9},{9,10},{10,11},{12,13},{... | collective-permute-start | bytes 92168 | tf_op jit(solution)/shard_map/ppermute | solution.py:17
  499.9 3.4 copy-start.29
  503.3 4.6 copy-start.16
  503.3 4.6 copy-start.19
  503.3 4.6 copy-start.23
  503.3 4.6 copy-start.24
  507.9 4.6 copy-start.2
  655.5 32.8 %copy-start.30 = (f32[128,64]{1,0:T(8,128)S(1)}, f32[128,64]{1,0:T(8,128)}, u32[]{:S(2)}) copy-start(f32[128,64]{1,0:T(8,128)} %pad_convert_fusion) | copy-start | bytes 98308
Sparse Core Ops, SparseCore 0:
  250.4 137.7 all-reduce.12
  512.7 142.8 all-reduce.10
where the time goes:
time: 752 us; the launch traced here: 744 us
  waiting for transfers between devices  318 us (42%)
  other arithmetic  146 us (19%)
  local copies, waits for them, and re-layouts  95.4 us (13%)
  starting transfers between devices  65.8 us (9%)
  matrix products  61.6 us (8%)
  blocking collectives  40.4 us (5%)
  between operations  16.8 us (2%)
    psum x2, waiting for transfers between devices, local(): lax.psum((gram_of(search_set, image_set), gram_of(search_set, mass_field...  266 us
    dot_general x27, matrix products, hidot(): jnp.dot(left, right, precision=lax.Precision.HIGHEST, preferred_element_t...  51.1 us
    ppermute x12, starting transfers between devices, with_halo(): before = lax.ppermute(last, axis, up)  50 us
    ppermute x12, waiting for transfers between devices, with_halo(): after = lax.ppermute(initial, axis, down)  46.2 us
    another operation x10, other arithmetic, ritz_filter(): factor = jnp.linalg.cholesky(pencil_m)  41.2 us
    psum x1, blocking collectives, start_sums(): lax.psum((gram_of(start_block, mass_field * start_block), gram_of(start_b...  40.4 us
    another operation x7, other arithmetic, lower_trans_solve(): lax.linalg.triangular_solve(lower_mat, rhs, left_side=True, lower=True, t...  30.2 us
    slice x7, local copies, waits for them, and re-layouts, with_halo(): initial = lax.slice_in_dim(x, 0, width, axis=dim)  24.8 us
  transfers between devices with their start and end apart: 26, of which 9 were waited for; matrix products, arithmetic and copies ran while one was open for 10% of the time, Pallas kernels for 0%

commit v1 on v0

--- a/solution.py
+++ b/solution.py
@@ -87,8 +87,11 @@
 
 def start_sums(start_block, mass_field, start_image, dof_count):
     mass_gram, stiff_gram = lax.psum(
-        (gram_of(start_block, mass_field * start_block), gram_of(start_block, start_image)),
-        ("gx", "gy", "gz"),
+        lax.psum(
+            (gram_of(start_block, mass_field * start_block), gram_of(start_block, start_image)),
+            "gx",
+        ),
+        ("gy", "gz"),
     )
     return (mass_gram / dof_count, stiff_gram / dof_count)
 

time: 752 us -> 756 us (level)
    psum x0 -> x1, blocking collectives: none -> 28.3 us  [start_sums(): lax.psum(lax.psum((gram_of(start_block, mass_field * start_block), gram_o...]
    psum x1, blocking collectives: 40.4 us -> 15.2 us  [start_sums(): lax.psum((gram_of(start_block, mass_field * start_block), gram_of(start_b...]
  transfers between devices with their start and end apart: 26 -> 26, of which waited for: 9 -> 10; matrix products, arithmetic and copies ran while one was open for 10% -> 10% of each run, Pallas kernels for 0% -> 0%
where the time goes in v1:
time: 756 us; the launch traced here: 749 us
  waiting for transfers between devices  319 us (42%)
  other arithmetic  146 us (19%)
  local copies, waits for them, and re-layouts  95.6 us (13%)
  starting transfers between devices  65.5 us (9%)
  matrix products  61.6 us (8%)
  blocking collectives  43.5 us (6%)
  between operations  16.8 us (2%)
    psum x2, waiting for transfers between devices, local(): lax.psum((gram_of(search_set, image_set), gram_of(search_set, mass_field...  267 us
    dot_general x27, matrix products, hidot(): jnp.dot(left, right, precision=lax.Precision.HIGHEST, preferred_element_t...  51.1 us
    ppermute x12, starting transfers between devices, with_halo(): before = lax.ppermute(last, axis, up)  49.7 us
    ppermute x12, waiting for transfers between devices, with_halo(): after = lax.ppermute(initial, axis, down)  46.2 us
    another operation x10, other arithmetic, ritz_filter(): factor = jnp.linalg.cholesky(pencil_m)  41.2 us
    another operation x7, other arithmetic, lower_trans_solve(): lax.linalg.triangular_solve(lower_mat, rhs, left_side=True, lower=True, t...  30.2 us
    psum x1, blocking collectives, start_sums(): lax.psum(lax.psum((gram_of(start_block, mass_field * start_block), gram_o...  28.3 us
    slice x7, local copies, waits for them, and re-layouts, with_halo(): initial = lax.slice_in_dim(x, 0, width, axis=dim)  24.8 us
  transfers between devices with their start and end apart: 26, of which 10 were waited for; matrix products, arithmetic and copies ran while one was open for 10% of the time, Pallas kernels for 0%

profile of v1, /device:TPU:0, one launch (start us, length us, event | category | flops | bytes accessed | tf_op | source)
XLA Modules:
  0.0 748.6 jit_solution(10120182862237928649)
XLA Ops:
  7.9 4.9 collective-permute-start
  17.3 5.4 collective-permute-start.7
  26.2 2.3 fusion.96
  33.0 5.4 collective-permute-done.7
  40.1 18.0 %collective-permute-done.6 = f32[64,3,1,8,128]{4,0,3,2,1:T(8,128)} collective-permute-done((f32[64,3,1,8,128]{4,0,3,2,1:T(8,128)}, f32[64,3,1,8,128]{4,0,3,2,1:T(8,128)}, u32[]{:S(2)}, u32[]{:S(2)}) %collective-permute-start.6) | collective-permute-done | bytes 786464 | tf_op jit(solution)/shard_map/ppermute | solution.py:18
  60.8 3.1 collective-permute-start.9
  64.0 3.5 collective-permute-start.4
  70.1 4.4 collective-permute-done.5
  76.6 4.4 fusion.183
  81.0 3.5 copy.129
  85.7 3.4 copy.131
  89.2 5.4 collective-permute-start.11
  96.3 3.5 copy.130
  99.8 3.3 copy.132
  103.2 5.7 fusion.61
  112.7 15.2 %all-reduce.8 = (f32[64,64]{0,1:T(8,128)S(1)}, f32[64,64]{0,1:T(8,128)S(1)}) all-reduce(f32[64,64]{0,1:T(8,128)S(1)} %copy-done.35, f32[64,64]{0,1:T(8,128)S(1)} %convolution_bitcast_fusion.3), channel_id=1, replica_groups=mesh['gx'=4,'gy'=2,'gz'=4] {'gx'}, use_global_device_ids=true, to_apply=%region_0.0 | all-reduce | flops 8192 | bytes 65536 | tf_op jit(solution)/shard_map/psum | solution.py:90
  127.9 28.3 %all-reduce.7 = (f32[64,64]{0,1:T(8,128)S(1)}, f32[64,64]{0,1:T(8,128)S(1)}) all-reduce(f32[64,64]{0,1:T(8,128)S(1)} %get-tuple-element.67, f32[64,64]{0,1:T(8,128)S(1)} %get-tuple-element.68), channel_id=1, replica_groups=mesh['gx'=4,'gy'=2,'gz'=4] {'gy','gz'}, use_global_device_ids=true, to_apply=%region_1.0 | all-reduce | flops 8192 | bytes 65536 | tf_op jit(solution)/shard_map/psum | solution.py:89
  156.3 5.8 cholesky.214
  163.5 4.9 custom-call.49
  172.4 3.2 subtract_divide_fusion
  177.1 3.3 fusion.179
  181.9 4.6 collective-permute-start.13
  186.6 16.4 %collective-permute-done.12 = f32[64,3,1,8,128]{4,0,3,2,1:T(8,128)S(1)} collective-permute-done((f32[64,3,1,8,128]{4,0,3,2,1:T(8,128)S(1)}, f32[64,3,1,8,128]{4,0,3,2,1:T(8,128)S(1)}, u32[]{:S(2)}, u32[]{:S(2)}) %collective-permute-start.12) | collective-permute-done | bytes 786464 | tf_op jit(solution)/shard_map/ppermute | solution.py:18
  204.9 3.3 collective-permute-start.15
  209.6 3.4 fusion.89
  214.2 4.4 fusion.182
  218.6 3.4 copy.142
  223.3 3.5 copy.144
  226.8 5.3 collective-permute-start.17
  235.9 3.5 copy.143
  239.4 3.3 copy.145
  242.7 4.3 fusion.47
  250.4 3.3 fusion.86
  253.8 3.9 maximum_bitcast_fusion.1
  257.7 4.0 copy.188
  263.2 129.2 %all-reduce.14.cloned.1.call-done = (f32[128,128]{0,1:T(8,128)}, f32[128,128]{0,1:T(8,128)}) async-done(((f32[128,128]{0,1:T(8,128)}, f32[128,128]{0,1:T(8,128)}), (f32[128,128]{0,1:T(8,128)}, f32[128,128]{0,1:T(8,128)})) %all-reduce.14.cloned.1.call-update) | async-done | bytes 131088 | tf_op jit(solution)/shard_map/psum | solution.py:135
  394.2 11.7 %cholesky.95 = f32[128,128]{1,0:T(8,128)S(1)} custom-call(f32[128,128]{1,0:T(8,128)S(1)} %fusion.124), custom_call_target="Cholesky" | custom-call | tf_op jit(solution)/shard_map/jit(cholesky)/cholesky | solution.py:73
  407.3 9.8 %custom-call.40 = f32[1,128,128]{1,2,0:T(8,128)S(1)} custom-call(f32[1,128,128]{2,1,0:T(8,128)S(1)} %get-tuple-element.103), custom_call_target="InvertDiagBlocksLowerTriangular" | custom-call | tf_op jit(solution)/shard_map/triangular_solve | solution.py:28
  422.7 5.8 cholesky.225
  429.9 4.9 custom-call.41
  441.1 5.9 fusion.177
  449.3 4.6 collective-permute-start.19
  456.7 2.7 copy_bitcast_fusion
  461.1 3.0 fusion.71
  464.1 6.2 collective-permute-done.18
  471.7 3.3 collective-permute-start.21
  475.0 4.8 fusion.83
  480.7 4.4 fusion.181
  485.1 3.4 copy.158
  489.8 3.4 copy.160
  493.2 5.2 collective-permute-start.23
  500.8 3.5 copy.159
  504.3 3.4 copy.161
  507.7 4.6 fusion.33
  512.3 4.6 fusion.80
  519.1 3.0 copy.203
  522.1 137.7 %all-reduce.12.cloned.1.call-done = (f32[192,192]{0,1:T(8,128)}, f32[192,192]{0,1:T(8,128)}) async-done(((f32[192,192]{0,1:T(8,128)}, f32[192,192]{0,1:T(8,128)}), (f32[192,192]{0,1:T(8,128)}, f32[192,192]{0,1:T(8,128)})) %all-reduce.12.cloned.1.call-update) | async-done | bytes 294928 | tf_op jit(solution)/shard_map/psum | solution.py:135
  662.0 11.7 %cholesky.155 = f32[128,128]{1,0:T(8,128)S(1)} custom-call(f32[128,128]{1,0:T(8,128)S(1)} %cholesky.245), custom_call_target="Cholesky" | custom-call | tf_op jit(solution)/shard_map/jit(cholesky)/cholesky | solution.py:73
  673.8 9.8 %custom-call.42 = f32[1,128,128]{1,2,0:T(8,128)S(1)} custom-call(f32[1,128,128]{2,1,0:T(8,128)S(1)} %get-tuple-element.101), custom_call_target="InvertDiagBlocksLowerTriangular" | custom-call | tf_op jit(solution)/shard_map/jit(cholesky)/cholesky | solution.py:73
  684.0 6.0 cholesky.169
  692.8 19.7 %custom-call.43 = f32[2,128,128]{1,2,0:T(8,128)S(1)} custom-call(f32[2,128,128]{2,1,0:T(8,128)S(1)} %pad_maximum_fusion.72), custom_call_target="InvertDiagBlocksLowerTriangular" | custom-call | tf_op jit(solution)/shard_map/triangular_solve | solution.py:28
  719.2 5.8 cholesky.236
  726.4 4.9 custom-call.44
  733.3 6.2 fusion.10
  (238 shorter events, 99.1 us)
Async XLA Ops:
  7.2 385.2 %all-reduce.14.cloned.1.call-start = ((), (), s32[]{:S(2)}) async-start(), calls=%async_computation.1 | async-start | bytes 262144 | tf_op jit(solution)/shard_map/psum | solution.py:135
  7.9 20.6 %collective-permute-start = (f32[3,2,8,128]{3,2,1,0:T(8,128)S(1)}, f32[3,2,8,128]{3,2,1,0:T(8,128)S(1)}, u32[]{:S(2)}, u32[]{:S(2)}) collective-permute-start(f32[3,2,8,128]{3,2,1,0:T(8,128)S(1)} %pad_maximum_fusion.78), channel_id=1, source_target_pairs={{0,8},{8,16},{16,24},{1,9},{9,17},{17,25},{2,10},{10,18},{18,26},{... | collective-permute-start | bytes 73736 | tf_op jit(solution)/shard_map/ppermute | solution.py:17
  12.8 15.7 %collective-permute-start.1 = (f32[3,2,8,128]{3,2,1,0:T(8,128)S(1)}, f32[3,2,8,128]{3,2,1,0:T(8,128)S(1)}, u32[]{:S(2)}, u32[]{:S(2)}) collective-permute-start(f32[3,2,8,128]{3,2,1,0:T(8,128)S(1)} %pad_maximum_fusion.78), channel_id=1, source_target_pairs={{8,0},{16,8},{24,16},{9,1},{17,9},{25,17},{10,2},{18,10},{26,18},{... | collective-permute-start | bytes 73736 | tf_op jit(solution)/shard_map/ppermute | solution.py:18
  16.0 8.1 %copy-start = (f32[64,3,2,8,128]{4,3,2,1,0:T(8,128)S(1)}, f32[64,3,2,8,128]{4,3,2,1,0:T(8,128)}, u32[]{:S(2)}) copy-start(f32[64,3,2,8,128]{4,3,2,1,0:T(8,128)} %param.13) | copy-start | bytes 4718596
  17.3 21.1 %collective-permute-start.7 = (f32[64,3,1,8,128]{4,0,3,2,1:T(8,128)}, f32[64,3,1,8,128]{4,0,3,2,1:T(8,128)}, u32[]{:S(2)}, u32[]{:S(2)}) collective-permute-start(f32[64,3,1,8,128]{4,0,3,2,1:T(8,128)} %get-tuple-element.93), channel_id=1, source_target_pairs={{0,8},{8,16},{16,24},{1,9},{9,17},{17,25},{2,10},{10,18},{18,26},{... | collective-permute-start | bytes 2359304 | tf_op jit(solution)/shard_map/ppermute | solution.py:17
  22.7 3.5 copy-start.26
  22.7 35.4 %collective-permute-start.6 = (f32[64,3,1,8,128]{4,0,3,2,1:T(8,128)}, f32[64,3,1,8,128]{4,0,3,2,1:T(8,128)}, u32[]{:S(2)}, u32[]{:S(2)}) collective-permute-start(f32[64,3,1,8,128]{4,0,3,2,1:T(8,128)} %get-tuple-element.92), channel_id=1, source_target_pairs={{8,0},{16,8},{24,16},{9,1},{17,9},{25,17},{10,2},{18,10},{26,18},{... | collective-permute-start | bytes 2359304 | tf_op jit(solution)/shard_map/ppermute | solution.py:18
  26.2 2.4 copy-start.27
  26.2 2.3 copy-start.28
  28.5 11.5 %copy-start.31 = (f32[3,2,8,128]{3,2,1,0:T(8,128)}, f32[3,2,8,128]{3,2,1,0:T(8,128)S(1)}, u32[]{:S(2)}) copy-start(f32[3,2,8,128]{3,2,1,0:T(8,128)S(1)} %collective-permute-done) | copy-start | bytes 73732
  28.6 11.5 %copy-start.33 = (f32[3,2,8,128]{3,2,1,0:T(8,128)}, f32[3,2,8,128]{3,2,1,0:T(8,128)S(1)}, u32[]{:S(2)}) copy-start(f32[3,2,8,128]{3,2,1,0:T(8,128)S(1)} %collective-permute-done.1) | copy-start | bytes 73732
  28.6 3.2 collective-permute-start.2
  29.9 3.1 collective-permute-start.3
  59.3 16.0 %copy-start.5 = (f32[64,3,4,8,128]{4,0,3,2,1:T(8,128)}, f32[64,3,4,8,128]{4,0,3,2,1:T(8,128)S(1)}, u32[]{:S(2)}) copy-start(f32[64,3,4,8,128]{4,0,3,2,1:T(8,128)S(1)} %constant_dynamic-update-slice_fusion) | copy-start | bytes 9437188
  59.3 15.2 %copy-start.32 = (f32[3,2,8,128]{3,2,1,0:T(8,128)S(1)}, f32[3,2,8,128]{3,2,1,0:T(8,128)}, u32[]{:S(2)}) copy-start(f32[3,2,8,128]{3,2,1,0:T(8,128)} %copy-done.31) | copy-start | bytes 73732
  59.3 15.2 %copy-start.34 = (f32[3,2,8,128]{3,2,1,0:T(8,128)S(1)}, f32[3,2,8,128]{3,2,1,0:T(8,128)}, u32[]{:S(2)}) copy-start(f32[3,2,8,128]{3,2,1,0:T(8,128)} %copy-done.33) | copy-start | bytes 73732
  59.4 15.9 %collective-permute-start.8 = (f32[64,3,4,1,128]{4,0,3,2,1:T(8,128)S(1)}, f32[64,3,4,1,128]{4,0,3,2,1:T(8,128)S(1)}, u32[]{:S(2)}, u32[]{:S(2)}) collective-permute-start(f32[64,3,4,1,128]{4,0,3,2,1:T(8,128)S(1)} %get-tuple-element.84), channel_id=1, source_target_pairs={{4,0},{5,1},{6,2},{7,3},{12,8},{13,9},{14,10},{15,11},{20,16},{21,... | collective-permute-start | bytes 1179656 | tf_op jit(solution)/shard_map/ppermute | solution.py:18
  60.8 14.5 %collective-permute-start.9 = (f32[64,3,4,1,128]{4,0,3,2,1:T(8,128)S(1)}, f32[64,3,4,1,128]{4,0,3,2,1:T(8,128)S(1)}, u32[]{:S(2)}, u32[]{:S(2)}) collective-permute-start(f32[64,3,4,1,128]{4,0,3,2,1:T(8,128)S(1)} %get-tuple-element.83), channel_id=1, source_target_pairs={{0,4},{1,5},{2,6},{3,7},{8,12},{9,13},{10,14},{11,15},{16,20},{17,... | collective-permute-start | bytes 1179656 | tf_op jit(solution)/shard_map/ppermute | solution.py:17
  64.0 6.1 collective-permute-start.4
  67.5 7.0 collective-permute-start.5
  75.3 0.8 copy-start.25
  84.5 11.9 %collective-permute-start.10 = (f32[64,3,4,10,1]{0,2,4,3,1:T(4,128)}, f32[64,3,4,10,1]{0,2,4,3,1:T(4,128)}, u32[]{:S(2)}, u32[]{:S(2)}) collective-permute-start(f32[64,3,4,10,1]{0,2,4,3,1:T(4,128)} %copy.129), channel_id=1, source_target_pairs={{1,0},{2,1},{3,2},{5,4},{6,5},{7,6},{9,8},{10,9},{11,10},{13,12},{... | collective-permute-start | bytes 92168 | tf_op jit(solution)/shard_map/ppermute | solution.py:18
  89.2 10.6 %collective-permute-start.11 = (f32[64,3,4,10,1]{0,2,4,3,1:T(4,128)}, f32[64,3,4,10,1]{0,2,4,3,1:T(4,128)}, u32[]{:S(2)}, u32[]{:S(2)}) collective-permute-start(f32[64,3,4,10,1]{0,2,4,3,1:T(4,128)} %copy.131), channel_id=1, source_target_pairs={{0,1},{1,2},{2,3},{4,5},{5,6},{6,7},{8,9},{9,10},{10,11},{12,13},{... | collective-permute-start | bytes 92168 | tf_op jit(solution)/shard_map/ppermute | solution.py:17
  110.7 2.1 copy-start.35
  170.8 1.5 copy-start.36
  170.8 1.6 copy-start.17
  175.6 1.3 copy-start.9
  180.6 22.3 %collective-permute-start.12 = (f32[64,3,1,8,128]{4,0,3,2,1:T(8,128)S(1)}, f32[64,3,1,8,128]{4,0,3,2,1:T(8,128)S(1)}, u32[]{:S(2)}, u32[]{:S(2)}) collective-permute-start(f32[64,3,1,8,128]{4,0,3,2,1:T(8,128)S(1)} %get-tuple-element.91), channel_id=1, source_target_pairs={{8,0},{16,8},{24,16},{9,1},{17,9},{25,17},{10,2},{18,10},{26,18},{... | collective-permute-start | bytes 2359304 | tf_op jit(solution)/shard_map/ppermute | solution.py:18
  181.9 21.6 %collective-permute-start.13 = (f32[64,3,1,8,128]{4,0,3,2,1:T(8,128)S(1)}, f32[64,3,1,8,128]{4,0,3,2,1:T(8,128)S(1)}, u32[]{:S(2)}, u32[]{:S(2)}) collective-permute-start(f32[64,3,1,8,128]{4,0,3,2,1:T(8,128)S(1)} %get-tuple-element.90), channel_id=1, source_target_pairs={{0,8},{8,16},{16,24},{1,9},{9,17},{17,25},{2,10},{10,18},{18,26},{... | collective-permute-start | bytes 2359304 | tf_op jit(solution)/shard_map/ppermute | solution.py:17
  203.0 10.1 %copy-start.11 = (f32[64,3,1,8,128]{4,0,3,2,1:T(8,128)}, f32[64,3,1,8,128]{4,0,3,2,1:T(8,128)S(1)}, u32[]{:S(2)}) copy-start(f32[64,3,1,8,128]{4,0,3,2,1:T(8,128)S(1)} %collective-permute-done.12) | copy-start | bytes 2359300
  203.6 9.5 %copy-start.12 = (f32[64,3,1,8,128]{4,0,3,2,1:T(8,128)}, f32[64,3,1,8,128]{4,0,3,2,1:T(8,128)S(1)}, u32[]{:S(2)}) copy-start(f32[64,3,1,8,128]{4,0,3,2,1:T(8,128)S(1)} %collective-permute-done.13) | copy-start | bytes 2359300
  203.6 9.4 %collective-permute-start.14 = (f32[64,3,4,1,128]{4,0,3,2,1:T(8,128)S(1)}, f32[64,3,4,1,128]{4,0,3,2,1:T(8,128)S(1)}, u32[]{:S(2)}, u32[]{:S(2)}) collective-permute-start(f32[64,3,4,1,128]{4,0,3,2,1:T(8,128)S(1)} %get-tuple-element.82), channel_id=1, source_target_pairs={{4,0},{5,1},{6,2},{7,3},{12,8},{13,9},{14,10},{15,11},{20,16},{21,... | collective-permute-start | bytes 1179656 | tf_op jit(solution)/shard_map/ppermute | solution.py:18
  204.9 8.1 %collective-permute-start.15 = (f32[64,3,4,1,128]{4,0,3,2,1:T(8,128)S(1)}, f32[64,3,4,1,128]{4,0,3,2,1:T(8,128)S(1)}, u32[]{:S(2)}, u32[]{:S(2)}) collective-permute-start(f32[64,3,4,1,128]{4,0,3,2,1:T(8,128)S(1)} %get-tuple-element.81), channel_id=1, source_target_pairs={{0,4},{1,5},{2,6},{3,7},{8,12},{9,13},{10,14},{11,15},{16,20},{17,... | collective-permute-start | bytes 1179656 | tf_op jit(solution)/shard_map/ppermute | solution.py:17
  209.6 3.4 copy-start.3
  213.1 0.7 copy-start.20
  222.1 13.8 %collective-permute-start.16 = (f32[64,3,4,10,1]{0,2,4,3,1:T(4,128)}, f32[64,3,4,10,1]{0,2,4,3,1:T(4,128)}, u32[]{:S(2)}, u32[]{:S(2)}) collective-permute-start(f32[64,3,4,10,1]{0,2,4,3,1:T(4,128)} %copy.142), channel_id=1, source_target_pairs={{1,0},{2,1},{3,2},{5,4},{6,5},{7,6},{9,8},{10,9},{11,10},{13,12},{... | collective-permute-start | bytes 92168 | tf_op jit(solution)/shard_map/ppermute | solution.py:18
  226.8 7.7 %copy-start.7 = (f32[64,6144]{1,0:T(8,128)S(1)}, f32[64,6144]{1,0:T(8,128)}, u32[]{:S(2)}) copy-start(f32[64,6144]{1,0:T(8,128)} %get-tuple-element.113) | copy-start | bytes 4718596
  226.8 12.6 %collective-permute-start.17 = (f32[64,3,4,10,1]{0,2,4,3,1:T(4,128)}, f32[64,3,4,10,1]{0,2,4,3,1:T(4,128)}, u32[]{:S(2)}, u32[]{:S(2)}) collective-permute-start(f32[64,3,4,10,1]{0,2,4,3,1:T(4,128)} %copy.144), channel_id=1, source_target_pairs={{0,1},{1,2},{2,3},{4,5},{5,6},{6,7},{8,9},{9,10},{10,11},{12,13},{... | collective-permute-start | bytes 92168 | tf_op jit(solution)/shard_map/ppermute | solution.py:17
  248.0 1.7 copy-start.4
  248.0 2.4 copy-start.18
  253.8 406.0 %all-reduce.12.cloned.1.call-start = ((), (), s32[]{:S(2)}) async-start(), calls=%async_computation | async-start | bytes 786432 | tf_op jit(solution)/shard_map/psum | solution.py:135
  257.7 4.0 copy-start.6
  263.2 172.4 %copy-start.8 = (f32[64,6144]{1,0:T(8,128)S(1)}, f32[64,6144]{1,0:T(8,128)}, u32[]{:S(2)}) copy-start(f32[64,6144]{1,0:T(8,128)} %get-tuple-element.113) | copy-start | bytes 4718596
  437.3 22.1 %copy-start.1 = (f32[64,6144]{1,0:T(8,128)}, f32[64,6144]{1,0:T(8,128)S(1)}, u32[]{:S(2)}) copy-start(f32[64,6144]{1,0:T(8,128)S(1)} %fusion.16) | copy-start | bytes 4718596
  437.5 2.0 copy-start.37
  439.2 1.9 copy-start.10
  447.1 6.8 copy-start.13
  448.0 22.3 %collective-permute-start.18 = (f32[64,3,1,8,128]{4,0,3,2,1:T(8,128)S(1)}, f32[64,3,1,8,128]{4,0,3,2,1:T(8,128)S(1)}, u32[]{:S(2)}, u32[]{:S(2)}) collective-permute-start(f32[64,3,1,8,128]{4,0,3,2,1:T(8,128)S(1)} %get-tuple-element.86), channel_id=1, source_target_pairs={{8,0},{16,8},{24,16},{9,1},{17,9},{25,17},{10,2},{18,10},{26,18},{... | collective-permute-start | bytes 2359304 | tf_op jit(solution)/shard_map/ppermute | solution.py:18
  449.3 21.0 %collective-permute-start.19 = (f32[64,3,1,8,128]{4,0,3,2,1:T(8,128)S(1)}, f32[64,3,1,8,128]{4,0,3,2,1:T(8,128)S(1)}, u32[]{:S(2)}, u32[]{:S(2)}) collective-permute-start(f32[64,3,1,8,128]{4,0,3,2,1:T(8,128)S(1)} %get-tuple-element.85), channel_id=1, source_target_pairs={{0,8},{8,16},{16,24},{1,9},{9,17},{17,25},{2,10},{10,18},{18,26},{... | collective-permute-start | bytes 2359304 | tf_op jit(solution)/shard_map/ppermute | solution.py:17
  455.8 19.2 %copy-start.15 = (f32[64,3,2,8,128]{4,0,3,2,1:T(8,128)}, f32[64,3,2,8,128]{4,0,3,2,1:T(8,128)S(1)}, u32[]{:S(2)}) copy-start(f32[64,3,2,8,128]{4,0,3,2,1:T(8,128)S(1)} %fusion.73) | copy-start | bytes 4718596
  459.7 1.4 copy-start.14
  460.2 14.8 %copy-start.22 = (f32[64,3,2,8,128]{4,0,3,2,1:T(8,128)}, f32[64,3,2,8,128]{4,0,3,2,1:T(8,128)S(1)}, u32[]{:S(2)}) copy-start(f32[64,3,2,8,128]{4,0,3,2,1:T(8,128)S(1)} %copy.155) | copy-start | bytes 4718596
  470.4 9.4 %collective-permute-start.20 = (f32[64,3,4,1,128]{4,0,3,2,1:T(8,128)S(1)}, f32[64,3,4,1,128]{4,0,3,2,1:T(8,128)S(1)}, u32[]{:S(2)}, u32[]{:S(2)}) collective-permute-start(f32[64,3,4,1,128]{4,0,3,2,1:T(8,128)S(1)} %get-tuple-element.80), channel_id=1, source_target_pairs={{4,0},{5,1},{6,2},{7,3},{12,8},{13,9},{14,10},{15,11},{20,16},{21,... | collective-permute-start | bytes 1179656 | tf_op jit(solution)/shard_map/ppermute | solution.py:18
  471.7 8.1 %collective-permute-start.21 = (f32[64,3,4,1,128]{4,0,3,2,1:T(8,128)S(1)}, f32[64,3,4,1,128]{4,0,3,2,1:T(8,128)S(1)}, u32[]{:S(2)}, u32[]{:S(2)}) collective-permute-start(f32[64,3,4,1,128]{4,0,3,2,1:T(8,128)S(1)} %get-tuple-element.79), channel_id=1, source_target_pairs={{0,4},{1,5},{2,6},{3,7},{8,12},{9,13},{10,14},{11,15},{16,20},{17,... | collective-permute-start | bytes 1179656 | tf_op jit(solution)/shard_map/ppermute | solution.py:17
  479.8 0.9 copy-start.21
  488.5 12.3 %collective-permute-start.22 = (f32[64,3,4,10,1]{0,2,4,3,1:T(4,128)}, f32[64,3,4,10,1]{0,2,4,3,1:T(4,128)}, u32[]{:S(2)}, u32[]{:S(2)}) collective-permute-start(f32[64,3,4,10,1]{0,2,4,3,1:T(4,128)} %copy.158), channel_id=1, source_target_pairs={{1,0},{2,1},{3,2},{5,4},{6,5},{7,6},{9,8},{10,9},{11,10},{13,12},{... | collective-permute-start | bytes 92168 | tf_op jit(solution)/shard_map/ppermute | solution.py:18
  493.2 11.0 %collective-permute-start.23 = (f32[64,3,4,10,1]{0,2,4,3,1:T(4,128)}, f32[64,3,4,10,1]{0,2,4,3,1:T(4,128)}, u32[]{:S(2)}, u32[]{:S(2)}) collective-permute-start(f32[64,3,4,10,1]{0,2,4,3,1:T(4,128)} %copy.160), channel_id=1, source_target_pairs={{0,1},{1,2},{2,3},{4,5},{5,6},{6,7},{8,9},{9,10},{10,11},{12,13},{... | collective-permute-start | bytes 92168 | tf_op jit(solution)/shard_map/ppermute | solution.py:17
  504.3 3.4 copy-start.29
  507.6 4.6 copy-start.16
  507.6 4.6 copy-start.19
  507.6 4.6 copy-start.23
  507.6 4.6 copy-start.24
  512.3 4.6 copy-start.2
  659.8 32.8 %copy-start.30 = (f32[128,64]{1,0:T(8,128)S(1)}, f32[128,64]{1,0:T(8,128)}, u32[]{:S(2)}) copy-start(f32[128,64]{1,0:T(8,128)} %pad_convert_fusion) | copy-start | bytes 98308
Sparse Core Ops, SparseCore 0:
  253.9 138.4 all-reduce.13
  517.0 142.7 all-reduce.11
